TPU v7x, 128 devices: a whole 4x4x4 slice. The times are simulated.
128 devices in a mesh: dev: 128 (over z, y, x, core).
Axes of the slice: x: 4, y: 4, z: 4, core: 2. Of those that a mesh axis runs over, the one named last changes fastest.
Arguments:
- embeddings: float32 [32768, 1024], P('dev'), may hold values from -6 to 6
- lists: int32 [32768], P('dev'), may hold values from 0 to 65535, as said below
- row_ids: int32 [32768], P('dev'), may hold values from 0 to 32767, each once
- centroids: float32 [65536, 1024], P('dev'), may hold values from -6 to 6
- rotation: float32 [1024, 1024], replicated, may hold values from -0.1875 to 0.1875
Outputs:
- packed: float32 [65536, 1024], P('dev')
- packed_ids: int32 [65536], P('dev')
- list_offsets: int32 [65536], P('dev')
Inputs may be any that keep to these rules, and one draw needn't show every extreme that they name: Lists l * 512 to (l + 1) * 512 - 1 belong to owner l. Among the rows of one device, at most 4 have lists of one owner, so an owner receives at most 512 rows; in every draw some owner receives exactly 4 rows from every device. `row_ids`: all identifiers are distinct.
All inputs are finite; a program needn't handle non-finite values.
Results may differ from a plain program's by a relative error of at most 0.0003.
Values sent between devices are 32-bit elements; how exact they have to be, the bound alone decides.
A program may use at most 64 MiB of HBM per device.

v0:
```python
import jax
import jax.numpy as jnp
from jax import lax
from jax.sharding import PartitionSpec as P


def place_rows(target, slot_total, values):
    table = jnp.arange(slot_total, dtype=jnp.int32)
    onehot = (target[None, :] == table[:, None]).astype(jnp.float32)
    return jnp.dot(
        onehot, values, precision=lax.Precision.HIGHEST, preferred_element_type=jnp.float32
    )


def place_ints(target, slot_total, values, filler):
    table = jnp.arange(slot_total, dtype=jnp.int32)
    match = target[None, :] == table[:, None]
    found = jnp.any(match, axis=1)
    picked = jnp.sum(jnp.where(match, values[None, :], 0), axis=1).astype(jnp.int32)
    return jnp.where(found, picked, filler)


def local(embeddings, lists, row_ids, centroids, rotation):
    row_count = lists.shape[0]
    feature_width = embeddings.shape[1]
    owned_lists = centroids.shape[0]
    device_count = lax.axis_size("dev")
    slot_count = 2 * row_count // device_count
    capacity = 2 * row_count
    owner_of = lists // owned_lists
    local_list = lists - owner_of * owned_lists
    row_index = jnp.arange(row_count, dtype=jnp.int32)
    earlier_mask = row_index[None, :] < row_index[:, None]
    list_rank = jnp.sum((lists[None, :] == lists[:, None]) & earlier_mask, axis=1)
    slot_rank = jnp.sum((owner_of[None, :] == owner_of[:, None]) & earlier_mask, axis=1)
    slot_total = slot_count * device_count
    flat_slot = slot_rank * device_count + owner_of
    send_rows = place_rows(flat_slot, slot_total, embeddings).reshape(
        slot_count, device_count, feature_width
    )
    send_lists = place_ints(flat_slot, slot_total, local_list, -1)
    send_second = place_ints(flat_slot, slot_total, list_rank, -1)
    send_ids = place_ints(flat_slot, slot_total, row_ids, -1)
    send_meta = jnp.stack([send_lists, send_second, send_ids], axis=-1).reshape(
        slot_count, device_count, 3
    )
    rows_in = lax.all_to_all(send_rows, "dev", split_axis=1, concat_axis=1, tiled=True)
    meta_in = lax.all_to_all(send_meta, "dev", split_axis=1, concat_axis=1, tiled=True)
    lists_in = meta_in[..., 0]
    is_valid = lists_in >= 0
    safe_list = jnp.maximum(lists_in, 0)
    centre_rows = centroids[safe_list]
    residual = jnp.where(is_valid[..., None], rows_in - centre_rows, 0.0)
    flat = residual.reshape(-1, feature_width)
    turned = jnp.dot(
        flat, rotation, precision=lax.Precision.HIGHEST, preferred_element_type=jnp.float32
    )
    turned, meta_got = (turned.reshape(residual.shape), meta_in)
    lists_got = meta_got[..., 0]
    second_got = meta_got[..., 1]
    ids_got = meta_got[..., 2]
    is_valid = lists_got >= 0
    safe_list = jnp.maximum(lists_got, 0)
    sources = jnp.broadcast_to(jnp.arange(device_count, dtype=jnp.int32)[None, :], lists_got.shape)
    flat_lists = lists_got.reshape(-1)
    flat_sources = sources.reshape(-1)
    list_table = jnp.arange(owned_lists, dtype=jnp.int32)
    total_mine = jnp.sum((flat_lists[:, None] == list_table[None, :]).astype(jnp.int32), axis=0)
    offsets = jnp.cumsum(total_mine) - total_mine
    same_list = flat_lists[None, :] == flat_lists[:, None]
    lower_source = flat_sources[None, :] < flat_sources[:, None]
    before_flat = jnp.sum((same_list & lower_source).astype(jnp.int32), axis=1)
    positions = offsets[safe_list] + before_flat.reshape(lists_got.shape) + second_got
    destination = jnp.where(is_valid, positions, capacity).reshape(-1).astype(jnp.int32)
    packed = place_rows(destination, capacity, turned.reshape(-1, feature_width))
    packed_ids = place_ints(destination, capacity, ids_got.reshape(-1), -1)
    return (packed, packed_ids, offsets)


def solution(mesh):
    in_specs = (P("dev", None), P("dev"), P("dev"), P("dev", None), P())
    out_specs = (P("dev", None), P("dev"), P("dev"))
    return jax.shard_map(local, mesh=mesh, in_specs=in_specs, out_specs=out_specs, check_vma=False)
```

profile of v0, /device:TPU:1, one launch (start us, length us, event | category | flops | bytes accessed | tf_op | source)
XLA Modules:
  0.0 76.7 jit_solution(7900835686559455578)
XLA Ops:
  0.6 0.0 copy-start
  0.6 1.0 %convert_reduce_fusion.2 = s32[256]{0:T(256)S(1)} fusion(s32[256]{0:T(256)} %param.6), kind=kLoop, calls=%fused_computation.18 | loop fusion | flops 327424 | bytes 2048 | tf_op jit(solution)/shard_map/reduce_sum | solution.py:34
  1.7 0.7 multiply_subtract_fusion
  2.4 0.2 convert_reduce_fusion.3
  2.6 0.2 fusion.5
  2.7 1.0 %select_reduce_fusion.3 = (s32[512]{0:T(512)S(1)}, s32[512]{0:T(512)S(1)}, s32[512]{0:T(512)S(1)}) fusion(s32[256]{0:T(256)S(1)} %get-tuple-element.8, s32[256]{0:T(256)S(1)} %multiply_add_fusion, s32[256]{0:T(256)} %param.7, s32[256]{0:T(256)S(1)} %convert_reduce_fusion.2), kind=kLoop, calls=%fused_computation.14 | loop fusion | flops 915968 | bytes 10240 | tf_op jit(solution)/shard_map/reduce_sum | solution.py:19
  3.8 0.9 %copy.26 = s32[4,128,3]{0,2,1:T(4,128)} copy(s32[4,128,3]{1,0,2:T(4,128)S(1)} %pad_add_fusion) | data formatting | bytes 12288 | tf_op jit(solution)/shard_map/stack | solution.py:44
  4.6 11.5 %all-to-all-start = ((s32[4,128,3]{0,2,1:T(4,128)}), s32[4,128,3]{0,2,1:T(4,128)S(1)}, u32[]{:S(2)}, u32[]{:S(2)}) async-start(s32[4,128,3]{0,2,1:T(4,128)} %copy.26), calls=%async_computation | async-start | bytes 524288 | tf_op jit(solution)/shard_map/all_to_all | solution.py:48
  16.1 2.3 %fusion.4 = f32[512,1024]{1,0:T(8,128)S(1)} fusion(f32[256,1024]{1,0:T(8,128)} %param.5, s32[256]{0:T(256)S(1)} %multiply_add_fusion), kind=kOutput, calls=%fused_computation.16 | convolution fusion | flops 1610743808 | bytes 3146752 | tf_op jit(solution)/shard_map/dot_general | solution.py:10
  18.4 2.6 %copy.29 = f32[4,128,1024]{2,0,1:T(4,128)} copy(f32[4,128,1024]{2,1,0:T(8,128)S(1)} %bitcast.31) | data formatting | bytes 4194304 | tf_op jit(solution)/shard_map/reshape | solution.py:38
  21.1 6.1 %all-to-all-done = s32[4,128,3]{0,2,1:T(4,128)S(1)} async-done(((s32[4,128,3]{0,2,1:T(4,128)}), s32[4,128,3]{0,2,1:T(4,128)S(1)}, u32[]{:S(2)}, u32[]{:S(2)}) %all-to-all-start) | async-done | bytes 6176 | tf_op jit(solution)/shard_map/all_to_all | solution.py:48
  27.2 5.2 %all-to-all-start.1 = ((f32[4,128,1024]{2,0,1:T(4,128)}), f32[4,128,1024]{2,0,1:T(4,128)}, u32[]{:S(2)}, u32[]{:S(2)}) async-start(f32[4,128,1024]{2,0,1:T(4,128)} %copy.29), calls=%async_computation.1 | async-start | bytes 4194304 | tf_op jit(solution)/shard_map/all_to_all | solution.py:47
  32.4 0.1 fusion.10
  32.6 0.1 copy.31
  32.6 0.1 copy.32
  32.7 0.1 copy.28
  32.8 0.5 convert_reduce_fusion
  33.3 0.3 reduce-window.9
  33.6 0.1 slice.18
  33.7 0.1 slice_reduce_fusion
  33.8 0.1 bitcast_subtract_fusion
  33.9 0.0 copy-start.1
  33.9 3.5 %gather_fusion = s32[512]{0:T(512)S(1)} fusion(s32[512]{0:T(512)S(1)} %bitcast_subtract_fusion, s32[1024]{0:T(1024)S(1)} %pad_clamp_fusion), kind=kCustom, calls=%fused_computation | custom fusion | bytes 6144 | tf_op jit(solution)/shard_map/gather | solution.py:73
  37.4 0.0 copy-done
  37.4 2.7 %gather_fusion.1 = f32[512,1024]{1,0:T(8,128)} fusion(f32[512,1024]{1,0:T(8,128)S(1)} %copy-done, s32[1024]{0:T(1024)S(1)} %pad_clamp_fusion), kind=kCustom, calls=%fused_computation.1 | custom fusion | bytes 4196352 | tf_op jit(solution)/shard_map/gather | solution.py:52
  40.1 0.0 copy-done.1
  40.1 0.2 fusion.1
  40.3 0.2 select_reduce_fusion
  40.5 0.6 broadcast_select_fusion
  41.0 21.6 %all-to-all-done.1 = f32[4,128,1024]{2,0,1:T(4,128)} async-done(((f32[4,128,1024]{2,0,1:T(4,128)}), f32[4,128,1024]{2,0,1:T(4,128)}, u32[]{:S(2)}, u32[]{:S(2)}) %all-to-all-start.1) | async-done | bytes 2097184 | tf_op jit(solution)/shard_map/all_to_all | solution.py:47
  62.6 0.0 copy-start.2
  62.6 3.8 %fusion = f32[4,128,1024]{2,1,0:T(8,128)S(1)} fusion(f32[4,128,1024]{2,1,0:T(8,128)} %bitcast.29, f32[4,128,1024]{2,0,1:T(4,128)} %all-to-all-done.1, pred[4,128]{1,0:T(4,128)(4,1)S(1)} %compare_bitcast_fusion), kind=kLoop, calls=%fused_computation.3 | loop fusion | flops 1048576 | bytes 6291968 | tf_op jit(solution)/shard_map/jit(_where)/select_n | solution.py:53
  66.4 0.0 copy-done.2
  66.5 6.9 %fusion.11 = f32[512,1024]{1,0:T(8,128)S(1)} fusion(f32[512,1024]{1,0:T(8,128)S(1)} %bitcast.30, f32[1024,1024]{1,0:T(8,128)S(1)} %copy-done.2), kind=kOutput, calls=%fused_computation.44 | convolution fusion | flops 6442450944 | bytes 8388608 | tf_op jit(solution)/shard_map/dot_general | solution.py:55
  73.4 3.3 %fusion.2 = f32[512,1024]{1,0:T(8,128)} fusion(f32[512,1024]{1,0:T(8,128)S(1)} %fusion.11, s32[512]{0:T(512)S(1)} %fusion.9), kind=kOutput, calls=%fused_computation.7 | convolution fusion | flops 3221487616 | bytes 4196352 | tf_op jit(solution)/shard_map/dot_general | solution.py:10
  (9 shorter events, 0.1 us)
Async XLA Ops:
  0.6 36.8 %copy-start = (f32[512,1024]{1,0:T(8,128)S(1)}, f32[512,1024]{1,0:T(8,128)}, u32[]{:S(2)}) copy-start(f32[512,1024]{1,0:T(8,128)} %param.8) | copy-start | bytes 6291460
  4.6 22.6 %all-to-all-start = ((s32[4,128,3]{0,2,1:T(4,128)}), s32[4,128,3]{0,2,1:T(4,128)S(1)}, u32[]{:S(2)}, u32[]{:S(2)}) async-start(s32[4,128,3]{0,2,1:T(4,128)} %copy.26), calls=%async_computation | async-start | bytes 524288 | tf_op jit(solution)/shard_map/all_to_all | solution.py:48
  27.2 35.4 %all-to-all-start.1 = ((f32[4,128,1024]{2,0,1:T(4,128)}), f32[4,128,1024]{2,0,1:T(4,128)}, u32[]{:S(2)}, u32[]{:S(2)}) async-start(f32[4,128,1024]{2,0,1:T(4,128)} %copy.29), calls=%async_computation.1 | async-start | bytes 4194304 | tf_op jit(solution)/shard_map/all_to_all | solution.py:47
  33.9 6.2 %copy-start.1 = (s32[512]{0:T(512)}, s32[512]{0:T(512)S(1)}, u32[]{:S(2)}) copy-start(s32[512]{0:T(512)S(1)} %bitcast_subtract_fusion) | copy-start | bytes 6148
  62.6 3.8 %copy-start.2 = (f32[1024,1024]{1,0:T(8,128)S(1)}, f32[1024,1024]{1,0:T(8,128)}, u32[]{:S(2)}) copy-start(f32[1024,1024]{1,0:T(8,128)} %param.9) | copy-start | bytes 12582916
where the time goes:
time: 77 us; the launch traced here: 76.7 us
  waiting for transfers between devices  27.7 us (36%)
  starting transfers between devices  16.7 us (22%)
  matrix products  12.5 us (16%)
  local copies, waits for them, and re-layouts  10.2 us (13%)
  other arithmetic  8.8 us (11%)
    all_to_all x1, waiting for transfers between devices, local(): lax.all_to_all(send_rows, 'dev', split_axis=1, concat_axis=1, tiled=True)  21.6 us
    all_to_all x1, starting transfers between devices, local(): lax.all_to_all(send_meta, 'dev', split_axis=1, concat_axis=1, tiled=True)  11.5 us
    dot_general x1, matrix products, local(): jnp.dot(flat, rotation, precision=lax.Precision.HIGHEST, preferred_elemen...  6.91 us
    all_to_all x1, waiting for transfers between devices, local(): lax.all_to_all(send_meta, 'dev', split_axis=1, concat_axis=1, tiled=True)  6.1 us
    dot_general x2, matrix products, place_rows(): jnp.dot(onehot, values, precision=lax.Precision.HIGHEST, preferred_elemen...  5.61 us
    all_to_all x1, starting transfers between devices, local(): lax.all_to_all(send_rows, 'dev', split_axis=1, concat_axis=1, tiled=True)  5.2 us
    select_n x1, other arithmetic, local(): residual = jnp.where(is_valid[..., None], rows_in - centre_rows, 0.0)  3.8 us
    gather x1, local copies, waits for them, and re-layouts, local(): offsets[safe_list] + before_flat.reshape(lists_got.shape) + second_got  3.49 us
  transfers between devices with their start and end apart: 2, of which 2 were waited for; matrix products, arithmetic and copies ran while one was open for 18% of the time, Pallas kernels for 0%

commit v1 on v0

v1 whole, which is shorter than its diff:
```python
import functools
import random

import jax
import jax.numpy as jnp
from jax import lax
from jax.experimental import pallas as pl
from jax.experimental.pallas import tpu as pltpu
from jax.sharding import PartitionSpec as P

MESH = pl.DeviceIdType.MESH
DIMS = (4, 4, 4, 2)
N = 128
SLOTS = 4
F32 = jnp.float32
BF16 = jnp.bfloat16
BIG = float(1 << 20)


def digits(k):
    return k // 32, k // 8 % 4, k // 2 % 4, k % 2


def hops(k):
    return sum((0, 1, 2, 1)[d] for d in digits(k)[:3])


def send_order():
    ks = list(range(1, N))
    random.Random(1).shuffle(ks)
    return sorted(ks, key=lambda k: -hops(k))


def iota(shape, dim):
    return lax.broadcasted_iota(jnp.int32, shape, dim)


def split3(x):
    hi = x.astype(BF16)
    rest = x - hi.astype(F32)
    mid = rest.astype(BF16)
    low = (rest - mid.astype(F32)).astype(BF16)
    return hi, mid, low


def split2(x):
    hi = x.astype(BF16)
    return hi, (x - hi.astype(F32)).astype(BF16)


def mm(a, b):
    return jnp.dot(a, b, preferred_element_type=F32)


def kernel(lists_ref, ids_ref, emb_hbm, cent_hbm, rot_hbm, packed_ref, pids_ref, offs_ref,
           emb, cent, rot, rot_hi, rot_lo, send, recv, msend, mrecv, cg, pos,
           lsem, ssem, rsem, msem):
    me = lax.axis_index("dev")
    emb_copy = pltpu.make_async_copy(emb_hbm, emb, lsem.at[0])
    cent_copy = pltpu.make_async_copy(cent_hbm, cent, lsem.at[1])
    rot_copy = pltpu.make_async_copy(rot_hbm, rot, lsem.at[2])
    emb_copy.start()
    cent_copy.start()
    rot_copy.start()

    barrier = pltpu.get_barrier_semaphore()
    for k in range(1, N):
        peer = me + k
        peer = jnp.where(peer >= N, peer - N, peer)
        pl.semaphore_signal(barrier, inc=1, device_id=(peer,), device_id_type=MESH)

    z, y, x, c = digits(me)
    zs = [((z + d) % 4) * 32 for d in range(4)]
    ys = [((y + d) % 4) * 8 for d in range(4)]
    xs = [((x + d) % 4) * 2 for d in range(4)]
    cs = [c, 1 - c]

    def peer_of(k):
        a, b, e, f = digits(k)
        return zs[a] + ys[b] + xs[e] + cs[f]

    order = send_order()

    rows = lists_ref.shape[1]
    owned = cent.shape[0]
    lists = lists_ref[...]
    owner = lists // owned
    local = (lists - owner * owned).astype(F32)
    ids = ids_ref[...].astype(F32)
    mine = owner == iota((N, rows), 0)
    earlier = (iota((rows, rows), 0) < iota((rows, rows), 1)).astype(BF16)
    count = mm(mine.astype(BF16), earlier)
    lane = iota((N, 128), 1)
    meta = jnp.zeros((N, 128), F32)
    picks = []
    for s in range(SLOTS):
        pick = mine & (count == float(s))
        l_of = jnp.sum(jnp.where(pick, local + 1.0, 0.0), axis=1, keepdims=True) - 1.0
        i_of = jnp.sum(jnp.where(pick, ids, 0.0), axis=1, keepdims=True)
        meta = jnp.where(lane == s, l_of, meta)
        meta = jnp.where(lane == SLOTS + s, i_of, meta)
        picks.append(pick.astype(BF16))
    msend[...] = meta.reshape(N, 1, 128)
    pick_all = jnp.concatenate(picks, axis=0)

    emb_copy.wait()
    width = emb.shape[1]
    for nb in range(width // 256):
        hi, mid, low = split3(emb[:, nb * 256:(nb + 1) * 256])
        out = mm(pick_all, hi) + mm(pick_all, mid) + mm(pick_all, low)
        for j in range(2):
            send[pl.ds(nb * 2 + j, SLOTS * N, stride=8), :] = out[:, j * 128:(j + 1) * 128]

    mrecv[pl.ds(me, 1)] = msend[pl.ds(me, 1)]
    for s in range(SLOTS):
        at = pl.ds(pl.multiple_of((s * N + me) * 8, 8), 8)
        recv[at, :] = send[at, :]

    pl.semaphore_wait(barrier, N - 1)
    for k in order:
        peer = peer_of(k)
        pltpu.make_async_remote_copy(
            src_ref=msend.at[pl.ds(peer, 1)], dst_ref=mrecv.at[pl.ds(me, 1)],
            send_sem=msem.at[0], recv_sem=msem.at[1], device_id=(peer,), device_id_type=MESH,
        ).start()

    def send_slot(s, carry):
        for k in order:
            peer = peer_of(k)
            pltpu.make_async_remote_copy(
                src_ref=send.at[pl.ds(pl.multiple_of((s * N + peer) * 8, 8), 8)],
                dst_ref=recv.at[pl.ds(pl.multiple_of((s * N + me) * 8, 8), 8)],
                send_sem=ssem.at[0], recv_sem=rsem.at[s], device_id=(peer,), device_id_type=MESH,
            ).start()
        return carry

    lax.fori_loop(0, SLOTS, send_slot, 0)

    rot_copy.wait()
    for nb in range(width // 256):
        at = slice(nb * 256, (nb + 1) * 256)
        hi, low = split2(rot[:, at])
        rot_hi[:, at] = hi
        rot_lo[:, at] = low

    m_all = msend.at[pl.ds(0, N - 1)]
    pltpu.make_async_copy(m_all, m_all, msem.at[1]).wait()
    got = mrecv[...].reshape(N, 128)
    got_t = got.T
    src_col = iota((N, 1), 0).astype(F32)
    src_row = iota((1, N), 1).astype(F32)
    list_cols = [got[:, s:s + 1] for s in range(SLOTS)]
    list_rows = [got_t[s:s + 1, :] for s in range(SLOTS)]

    def keys(lists_of, src):
        return [jnp.where(v >= 0, v * float(SLOTS * N) + src * float(SLOTS) + float(s), BIG)
                for s, v in enumerate(lists_of)]

    key_cols = keys(list_cols, src_col)
    key_rows = keys(list_rows, src_row)
    q_lane = iota((N, owned), 1).astype(F32)
    pid = jnp.zeros((1, owned), F32)
    off = jnp.zeros((1, owned), F32)
    for s in range(SLOTS):
        by_row = jnp.zeros((N, N), F32)
        by_col = jnp.zeros((N, N), F32)
        for t in range(SLOTS):
            by_row += (key_cols[t] < key_rows[s]).astype(F32)
            by_col += (key_rows[t] < key_cols[s]).astype(F32)
        at_row = jnp.where(list_rows[s] >= 0, jnp.sum(by_row, axis=0, keepdims=True), BIG)
        at_col = jnp.where(list_cols[s] >= 0, jnp.sum(by_col, axis=1, keepdims=True), BIG)
        pos[s:s + 1, :] = at_row
        id_col = got[:, SLOTS + s:SLOTS + s + 1] + 1.0
        pid += jnp.sum(jnp.where(at_col == q_lane, id_col, 0.0), axis=0, keepdims=True)
        off += jnp.sum((key_cols[s] < q_lane * float(SLOTS * N)).astype(F32), axis=0, keepdims=True)
    pids_ref[...] = (pid - 1.0).astype(jnp.int32)
    offs_ref[...] = off.astype(jnp.int32)

    cent_copy.wait()
    onehot = jnp.concatenate([(v == q_lane).astype(BF16) for v in list_cols], axis=0)
    for nb in range(width // 256):
        hi, mid, low = split3(cent[:, nb * 256:(nb + 1) * 256])
        cg[:, nb * 256:(nb + 1) * 256] = mm(onehot, hi) + mm(onehot, mid) + mm(onehot, low)

    packed_ref[...] = jnp.zeros(packed_ref.shape, F32)
    q_sub = iota((SLOTS * N, N), 0).astype(F32)

    def chunk(s, carry):
        r_all = recv.at[pl.ds(0, (N - 1) * 8)]
        pltpu.make_async_copy(r_all, r_all, rsem.at[s]).wait()
        parts = [recv[pl.ds(s * (N * 8) + j, N, stride=8), :] for j in range(8)]
        resid = jnp.concatenate(parts, axis=1) - cg[pl.ds(pl.multiple_of(s * N, N), N), :]
        hi, low = split2(resid)
        both = jnp.concatenate([hi, low], axis=0)
        place = (pos[pl.ds(s, 1), :] == q_sub).astype(BF16)
        place2 = jnp.concatenate([place, place], axis=1)
        for nb in range(width // 256):
            at = slice(nb * 256, (nb + 1) * 256)
            first = mm(both, rot_hi[:, at])
            turned = first[:N] + first[N:] + mm(hi, rot_lo[:, at])
            t_hi, t_lo = split2(turned)
            packed_ref[:, at] += mm(place2, jnp.concatenate([t_hi, t_lo], axis=0))
        return carry

    lax.fori_loop(0, SLOTS, chunk, 0)
    s_all = send.at[pl.ds(0, SLOTS * (N - 1) * 8)]
    pltpu.make_async_copy(s_all, s_all, ssem.at[0]).wait()
    pltpu.make_async_copy(m_all, m_all, msem.at[0]).wait()


def local(embeddings, lists, row_ids, centroids, rotation):
    rows, width = embeddings.shape
    owned = centroids.shape[0]
    slots = SLOTS * N
    vm = pl.BlockSpec(memory_space=pltpu.VMEM)
    hbm = pl.BlockSpec(memory_space=pl.ANY)
    packed, pids, offs = pl.pallas_call(
        kernel,
        name="exchange",
        out_shape=(
            jax.ShapeDtypeStruct((slots, width), F32),
            jax.ShapeDtypeStruct((1, slots), jnp.int32),
            jax.ShapeDtypeStruct((1, owned), jnp.int32),
        ),
        in_specs=[vm, vm, hbm, hbm, hbm],
        out_specs=(vm, vm, vm),
        scratch_shapes=[
            pltpu.VMEM((rows, width), F32),
            pltpu.VMEM((owned, width), F32),
            pltpu.VMEM((width, width), F32),
            pltpu.VMEM((width, width), BF16),
            pltpu.VMEM((width, width), BF16),
            pltpu.VMEM((slots * 8, 128), F32),
            pltpu.VMEM((slots * 8, 128), F32),
            pltpu.VMEM((N, 1, 128), F32),
            pltpu.VMEM((N, 1, 128), F32),
            pltpu.VMEM((slots, width), F32),
            pltpu.VMEM((8, 128), F32),
            pltpu.SemaphoreType.DMA((3,)),
            pltpu.SemaphoreType.DMA((1,)),
            pltpu.SemaphoreType.DMA((SLOTS,)),
            pltpu.SemaphoreType.DMA((2,)),
        ],
        compiler_params=pltpu.CompilerParams(
            collective_id=0, has_side_effects=True, vmem_limit_bytes=40 << 20
        ),
    )(lists.reshape(1, rows), row_ids.reshape(1, rows), embeddings, centroids, rotation)
    return packed, pids.reshape(-1), offs.reshape(-1)


def solution(mesh):
    in_specs = (P("dev", None), P("dev"), P("dev"), P("dev", None), P())
    out_specs = (P("dev", None), P("dev"), P("dev"))
    return jax.shard_map(local, mesh=mesh, in_specs=in_specs, out_specs=out_specs, check_vma=False)
```

time: 77 us -> 49.6 us (0.64)
  Pallas kernels: 0 us -> 39.9 us
  waiting for transfers between devices: 27.7 us -> 0 us
  starting transfers between devices: 16.7 us -> 0 us
  matrix products: 12.5 us -> 0 us
  other arithmetic: 8.8 us -> 0 us
  local copies, waits for them, and re-layouts: 10.2 us -> 8.83 us
    pallas_call x0 -> x1, Pallas kernels: none -> 39.9 us  [local(): pl.pallas_call(kernel, name='exchange', out_shape=(jax.ShapeDtypeStruct((...]
    all_to_all x2 -> x0, waiting for transfers between devices: 27.7 us -> none  [the longest x1 21.6 us: local(): lax.all_to_all(send_rows, 'dev', split_axis=1, concat_axis=1, tiled=True)]
    all_to_all x2 -> x0, starting transfers between devices: 16.7 us -> none  [the longest x1 11.5 us: local(): lax.all_to_all(send_meta, 'dev', split_axis=1, concat_axis=1, tiled=True)]
    dot_general x3 -> x0, matrix products: 12.5 us -> none  [the longest x1 6.91 us: local(): jnp.dot(flat, rotation, precision=lax.Precision.HIGHEST, preferred_elemen...]
    unnamed x7 -> x13, local copies, waits for them, and re-layouts: 0.09 us -> 8.83 us
    gather x2 -> x0, local copies, waits for them, and re-layouts: 6.14 us -> none  [the longest x1 3.49 us: local(): offsets[safe_list] + before_flat.reshape(lists_got.shape) + second_got]
    select_n x4 -> x0, other arithmetic: 4.39 us -> none  [the longest x1 3.8 us: local(): residual = jnp.where(is_valid[..., None], rows_in - centre_rows, 0.0)]
    reduce_sum x5 -> x0, other arithmetic: 2.92 us -> none  [the longest x2 1.21 us: place_ints(): jnp.sum(jnp.where(match, values[None, :], 0), axis=1).astype(jnp.int32)]
  transfers between devices with their start and end apart: 2 -> 0, of which waited for: 2 -> 0; matrix products, arithmetic and copies ran while one was open for 18% -> 0% of each run, Pallas kernels for 0% -> 0%
where the time goes in v1:
time: 49.6 us; the launch traced here: 49.4 us
  Pallas kernels  39.9 us (80%)
  local copies, waits for them, and re-layouts  8.83 us (18%)
  between operations  0.65 us (1%)
    pallas_call x1, Pallas kernels, local(): pl.pallas_call(kernel, name='exchange', out_shape=(jax.ShapeDtypeStruct((...  39.9 us
    unnamed x13, local copies, waits for them, and re-layouts  8.83 us

profile of v1, /device:TPU:1, one launch (start us, length us, event | category | flops | bytes accessed | tf_op | source)
XLA Modules:
  0.0 49.4 jit_solution(9225061103760199300)
XLA Ops:
  0.6 0.0 copy-start
  0.6 2.2 %copy-done = f32[1024,1024]{1,0:T(8,128)S(1)} copy-done((f32[1024,1024]{1,0:T(8,128)S(1)}, f32[1024,1024]{1,0:T(8,128)}, u32[]{:S(2)}) %copy-start) | copy-done | bytes 4194328
  2.8 0.0 copy-start.1
  2.8 1.6 %copy-done.1 = f32[512,1024]{1,0:T(8,128)S(1)} copy-done((f32[512,1024]{1,0:T(8,128)S(1)}, f32[512,1024]{1,0:T(8,128)}, u32[]{:S(2)}) %copy-start.1) | copy-done | bytes 2097176
  4.4 0.0 copy-start.2
  4.4 1.2 %copy-done.2 = f32[256,1024]{1,0:T(8,128)S(1)} copy-done((f32[256,1024]{1,0:T(8,128)S(1)}, f32[256,1024]{1,0:T(8,128)}, u32[]{:S(2)}) %copy-start.2) | copy-done | bytes 1048600
  5.6 0.0 copy-start.3
  5.6 0.7 %copy-done.3 = s32[256]{0:T(256)S(1)} copy-done((s32[256]{0:T(256)S(1)}, s32[256]{0:T(256)}, u32[]{:S(2)}) %copy-start.3) | copy-done | bytes 1048
  6.3 0.0 copy-start.4
  6.3 0.7 %copy-done.4 = s32[256]{0:T(256)S(1)} copy-done((s32[256]{0:T(256)S(1)}, s32[256]{0:T(256)}, u32[]{:S(2)}) %copy-start.4) | copy-done | bytes 1048
  7.0 39.9 %exchange.1 = (f32[512,1024]{1,0:T(8,128)S(1)}, s32[1,512]{1,0:T(1,128)S(1)}, s32[1,512]{1,0:T(1,128)S(1)}) custom-call(s32[1,256]{1,0:T(1,128)S(1)} %bitcast.6, s32[1,256]{1,0:T(1,128)S(1)} %bitcast.7, f32[256,1024]{1,0:T(8,128)S(1)} %copy-done.2, f32[512,1024]{1,0:T(8,128)S(1)} %copy-done.1, f32[1024,1024]{1,0:T(8,128)S(1)} %copy-done), custom_call_target="tpu_custom_call" | custom-call | tf_op jit(solution)/shard_map/exchange/pallas_call | solution.py:217
  46.9 1.3 %copy.11 = f32[512,1024]{1,0:T(8,128)} copy(f32[512,1024]{1,0:T(8,128)S(1)} %get-tuple-element.12) | data formatting | bytes 4194304
  48.2 0.6 %copy.12 = s32[512]{0:T(512)} copy(s32[512]{0:T(512)S(1)} %bitcast.5) | data formatting | bytes 4096
  48.8 0.6 %copy.13 = s32[512]{0:T(512)} copy(s32[512]{0:T(512)S(1)} %bitcast.4) | data formatting | bytes 4096
Async XLA Ops:
  0.6 2.2 %copy-start = (f32[1024,1024]{1,0:T(8,128)S(1)}, f32[1024,1024]{1,0:T(8,128)}, u32[]{:S(2)}) copy-start(f32[1024,1024]{1,0:T(8,128)} %rot_hbm.1) | copy-start | bytes 12582916
  2.8 1.6 %copy-start.1 = (f32[512,1024]{1,0:T(8,128)S(1)}, f32[512,1024]{1,0:T(8,128)}, u32[]{:S(2)}) copy-start(f32[512,1024]{1,0:T(8,128)} %cent_hbm.1) | copy-start | bytes 6291460
  4.4 1.2 %copy-start.2 = (f32[256,1024]{1,0:T(8,128)S(1)}, f32[256,1024]{1,0:T(8,128)}, u32[]{:S(2)}) copy-start(f32[256,1024]{1,0:T(8,128)} %emb_hbm.1) | copy-start | bytes 3145732
  5.6 0.7 %copy-start.3 = (s32[256]{0:T(256)S(1)}, s32[256]{0:T(256)}, u32[]{:S(2)}) copy-start(s32[256]{0:T(256)} %param.6) | copy-start | bytes 3076
  6.3 0.7 %copy-start.4 = (s32[256]{0:T(256)S(1)}, s32[256]{0:T(256)}, u32[]{:S(2)}) copy-start(s32[256]{0:T(256)} %param.7) | copy-start | bytes 3076

commit v2 on v1

--- a/solution.py
+++ b/solution.py
@@ -52,16 +52,18 @@
     return jnp.dot(a, b, preferred_element_type=F32)
 
 
-def kernel(lists_ref, ids_ref, emb_hbm, cent_hbm, rot_hbm, packed_ref, pids_ref, offs_ref,
-           emb, cent, rot, rot_hi, rot_lo, send, recv, msend, mrecv, cg, pos,
+def kernel(lists_hbm, ids_hbm, emb_hbm, cent_hbm, rot_hbm, packed_ref, pids_ref, offs_ref,
+           lists_ref, ids_ref, emb, cent, rot, rot_hi, rot_lo, send, recv, msend, mrecv, cg, pos,
            lsem, ssem, rsem, msem):
     me = lax.axis_index("dev")
+    lists_copy = pltpu.make_async_copy(lists_hbm, lists_ref, lsem.at[3])
+    ids_copy = pltpu.make_async_copy(ids_hbm, ids_ref, lsem.at[4])
     emb_copy = pltpu.make_async_copy(emb_hbm, emb, lsem.at[0])
     cent_copy = pltpu.make_async_copy(cent_hbm, cent, lsem.at[1])
     rot_copy = pltpu.make_async_copy(rot_hbm, rot, lsem.at[2])
+    lists_copy.start()
+    ids_copy.start()
     emb_copy.start()
-    cent_copy.start()
-    rot_copy.start()
 
     barrier = pltpu.get_barrier_semaphore()
     for k in range(1, N):
@@ -83,6 +85,8 @@
 
     rows = lists_ref.shape[1]
     owned = cent.shape[0]
+    lists_copy.wait()
+    ids_copy.wait()
     lists = lists_ref[...]
     owner = lists // owned
     local = (lists - owner * owned).astype(F32)
@@ -104,6 +108,8 @@
     pick_all = jnp.concatenate(picks, axis=0)
 
     emb_copy.wait()
+    rot_copy.start()
+    cent_copy.start()
     width = emb.shape[1]
     for nb in range(width // 256):
         hi, mid, low = split3(emb[:, nb * 256:(nb + 1) * 256])
@@ -208,23 +214,39 @@
     pltpu.make_async_copy(m_all, m_all, msem.at[0]).wait()
 
 
+def write_out(packed_vm, pids_vm, offs_vm, packed_ref, pids_ref, offs_ref, sem):
+    pairs = ((packed_vm, packed_ref), (pids_vm, pids_ref), (offs_vm, offs_ref))
+    copies = [pltpu.make_async_copy(a, b, sem.at[i]) for i, (a, b) in enumerate(pairs)]
+    for copy in copies:
+        copy.start()
+    for copy in copies:
+        copy.wait()
+
+
 def local(embeddings, lists, row_ids, centroids, rotation):
     rows, width = embeddings.shape
     owned = centroids.shape[0]
     slots = SLOTS * N
     vm = pl.BlockSpec(memory_space=pltpu.VMEM)
-    hbm = pl.BlockSpec(memory_space=pl.ANY)
-    packed, pids, offs = pl.pallas_call(
+    hbm = pl.BlockSpec(memory_space=pltpu.HBM)
+    results = (
+        jax.ShapeDtypeStruct((slots, width), F32),
+        jax.ShapeDtypeStruct((1, slots), jnp.int32),
+        jax.ShapeDtypeStruct((1, owned), jnp.int32),
+    )
+    in_hbm = [
+        pltpu.with_memory_space_constraint(v, pltpu.HBM)
+        for v in (lists.reshape(1, rows), row_ids.reshape(1, rows), embeddings, centroids, rotation)
+    ]
+    held = pl.pallas_call(
         kernel,
         name="exchange",
-        out_shape=(
-            jax.ShapeDtypeStruct((slots, width), F32),
-            jax.ShapeDtypeStruct((1, slots), jnp.int32),
-            jax.ShapeDtypeStruct((1, owned), jnp.int32),
-        ),
-        in_specs=[vm, vm, hbm, hbm, hbm],
+        out_shape=results,
+        in_specs=[hbm] * 5,
         out_specs=(vm, vm, vm),
         scratch_shapes=[
+            pltpu.VMEM((1, rows), jnp.int32),
+            pltpu.VMEM((1, rows), jnp.int32),
             pltpu.VMEM((rows, width), F32),
             pltpu.VMEM((owned, width), F32),
             pltpu.VMEM((width, width), F32),
@@ -236,7 +258,7 @@
             pltpu.VMEM((N, 1, 128), F32),
             pltpu.VMEM((slots, width), F32),
             pltpu.VMEM((8, 128), F32),
-            pltpu.SemaphoreType.DMA((3,)),
+            pltpu.SemaphoreType.DMA((5,)),
             pltpu.SemaphoreType.DMA((1,)),
             pltpu.SemaphoreType.DMA((SLOTS,)),
             pltpu.SemaphoreType.DMA((2,)),
@@ -244,7 +266,16 @@
         compiler_params=pltpu.CompilerParams(
             collective_id=0, has_side_effects=True, vmem_limit_bytes=40 << 20
         ),
-    )(lists.reshape(1, rows), row_ids.reshape(1, rows), embeddings, centroids, rotation)
+    )(*in_hbm)
+    packed, pids, offs = pl.pallas_call(
+        write_out,
+        name="write_out",
+        out_shape=results,
+        in_specs=[vm] * 3,
+        out_specs=(hbm,) * 3,
+        scratch_shapes=[pltpu.SemaphoreType.DMA((3,))],
+        compiler_params=pltpu.CompilerParams(vmem_limit_bytes=4 << 20),
+    )(*held)
     return packed, pids.reshape(-1), offs.reshape(-1)
 
 

time: 49.6 us -> 41.5 us (0.84)
  local copies, waits for them, and re-layouts: 8.83 us -> 0 us
  Pallas kernels: 39.9 us -> 40.8 us
    unnamed x13 -> x0, local copies, waits for them, and re-layouts: 8.83 us -> none
    pallas_call x1 -> x2, Pallas kernels: 39.9 us -> 40.8 us  [the longest x1 39.4 us: local(): pl.pallas_call(kernel, name='exchange', out_shape=results, in_specs=[hbm]...]
where the time goes in v2:
time: 41.5 us; the launch traced here: 41.4 us
  Pallas kernels  40.8 us (98%)
  between operations  0.64 us (2%)
    pallas_call x1, Pallas kernels, local(): pl.pallas_call(kernel, name='exchange', out_shape=results, in_specs=[hbm]...  39.4 us
    pallas_call x1, Pallas kernels, local(): pl.pallas_call(write_out, name='write_out', out_shape=results, in_specs=[...  1.35 us

profile of v2, /device:TPU:1, one launch (start us, length us, event | category | flops | bytes accessed | tf_op | source)
XLA Modules:
  0.0 41.4 jit_solution(12375672328894540454)
XLA Ops:
  0.6 39.4 %exchange.1 = (f32[512,1024]{1,0:T(8,128)S(1)}, s32[1,512]{1,0:T(1,128)S(1)}, s32[1,512]{1,0:T(1,128)S(1)}) custom-call(s32[1,256]{1,0:T(1,128)} %bitcast.4, s32[1,256]{1,0:T(1,128)} %bitcast.5, f32[256,1024]{1,0:T(8,128)} %emb_hbm.1, f32[512,1024]{1,0:T(8,128)} %cent_hbm.1, f32[1024,1024]{1,0:T(8,128)} %rot_hbm.1), custom_call_target="tpu_custom_call" | custom-call | tf_op jit(solution)/shard_map/exchange/pallas_call | solution.py:241
  40.0 1.4 %write_out.1 = (f32[512,1024]{1,0:T(8,128)}, s32[1,512]{1,0:T(1,128)}, s32[1,512]{1,0:T(1,128)}) custom-call(f32[512,1024]{1,0:T(8,128)S(1)} %get-tuple-element.9.packed_vm, s32[1,512]{1,0:T(1,128)S(1)} %get-tuple-element.10.pids_vm, s32[1,512]{1,0:T(1,128)S(1)} %get-tuple-element.11.offs_vm), custom_call_target="tpu_custom_call" | custom-call | tf_op jit(solution)/shard_map/write_out/pallas_call | solution.py:270

commit v3 on v2

--- a/solution.py
+++ b/solution.py
@@ -53,7 +53,7 @@
 
 
 def kernel(lists_hbm, ids_hbm, emb_hbm, cent_hbm, rot_hbm, packed_ref, pids_ref, offs_ref,
-           lists_ref, ids_ref, emb, cent, rot, rot_hi, rot_lo, send, recv, msend, mrecv, cg, pos,
+           lists_ref, ids_ref, emb, cent, rot, rot_hi, rot_lo, send, recv, msend, mrecv, cg, pos, turned2,
            lsem, ssem, rsem, msem):
     me = lax.axis_index("dev")
     lists_copy = pltpu.make_async_copy(lists_hbm, lists_ref, lsem.at[3])
@@ -205,7 +205,9 @@
             first = mm(both, rot_hi[:, at])
             turned = first[:N] + first[N:] + mm(hi, rot_lo[:, at])
             t_hi, t_lo = split2(turned)
-            packed_ref[:, at] += mm(place2, jnp.concatenate([t_hi, t_lo], axis=0))
+            turned2[0:N, at] = t_hi
+            turned2[N:, at] = t_lo
+        packed_ref[...] += mm(place2, turned2[...])
         return carry
 
     lax.fori_loop(0, SLOTS, chunk, 0)
@@ -258,6 +260,7 @@
             pltpu.VMEM((N, 1, 128), F32),
             pltpu.VMEM((slots, width), F32),
             pltpu.VMEM((8, 128), F32),
+            pltpu.VMEM((2 * N, width), BF16),
             pltpu.SemaphoreType.DMA((5,)),
             pltpu.SemaphoreType.DMA((1,)),
             pltpu.SemaphoreType.DMA((SLOTS,)),

time: 41.5 us -> 39.9 us (0.961)
  Pallas kernels: 40.8 us -> 39.2 us
    pallas_call x1, Pallas kernels: 39.4 us -> 37.8 us  [local(): pl.pallas_call(kernel, name='exchange', out_shape=results, in_specs=[hbm]...]
where the time goes in v3:
time: 39.9 us; the launch traced here: 39.8 us
  Pallas kernels  39.2 us (98%)
  between operations  0.64 us (2%)
    pallas_call x1, Pallas kernels, local(): pl.pallas_call(kernel, name='exchange', out_shape=results, in_specs=[hbm]...  37.8 us
    pallas_call x1, Pallas kernels, local(): pl.pallas_call(write_out, name='write_out', out_shape=results, in_specs=[...  1.35 us

profile of v3, /device:TPU:1, one launch (start us, length us, event | category | flops | bytes accessed | tf_op | source)
XLA Modules:
  0.0 39.8 jit_solution(12169578683280626544)
XLA Ops:
  0.6 37.8 %exchange.1 = (f32[512,1024]{1,0:T(8,128)S(1)}, s32[1,512]{1,0:T(1,128)S(1)}, s32[1,512]{1,0:T(1,128)S(1)}) custom-call(s32[1,256]{1,0:T(1,128)} %bitcast.4, s32[1,256]{1,0:T(1,128)} %bitcast.5, f32[256,1024]{1,0:T(8,128)} %emb_hbm.1, f32[512,1024]{1,0:T(8,128)} %cent_hbm.1, f32[1024,1024]{1,0:T(8,128)} %rot_hbm.1), custom_call_target="tpu_custom_call" | custom-call | tf_op jit(solution)/shard_map/exchange/pallas_call | solution.py:243
  38.4 1.4 %write_out.1 = (f32[512,1024]{1,0:T(8,128)}, s32[1,512]{1,0:T(1,128)}, s32[1,512]{1,0:T(1,128)}) custom-call(f32[512,1024]{1,0:T(8,128)S(1)} %get-tuple-element.9.packed_vm, s32[1,512]{1,0:T(1,128)S(1)} %get-tuple-element.10.pids_vm, s32[1,512]{1,0:T(1,128)S(1)} %get-tuple-element.11.offs_vm), custom_call_target="tpu_custom_call" | custom-call | tf_op jit(solution)/shard_map/write_out/pallas_call | solution.py:273

commit v4 on v3

--- a/solution.py
+++ b/solution.py
@@ -15,6 +15,7 @@
 F32 = jnp.float32
 BF16 = jnp.bfloat16
 BIG = float(1 << 20)
+NEAR_SLOTS = 3
 
 
 def digits(k):
@@ -54,7 +55,7 @@
 
 def kernel(lists_hbm, ids_hbm, emb_hbm, cent_hbm, rot_hbm, packed_ref, pids_ref, offs_ref,
            lists_ref, ids_ref, emb, cent, rot, rot_hi, rot_lo, send, recv, msend, mrecv, cg, pos, turned2,
-           lsem, ssem, rsem, msem):
+           lsem, ssem, rsem, msem, wider):
     me = lax.axis_index("dev")
     lists_copy = pltpu.make_async_copy(lists_hbm, lists_ref, lsem.at[3])
     ids_copy = pltpu.make_async_copy(ids_hbm, ids_ref, lsem.at[4])
@@ -65,12 +66,6 @@
     ids_copy.start()
     emb_copy.start()
 
-    barrier = pltpu.get_barrier_semaphore()
-    for k in range(1, N):
-        peer = me + k
-        peer = jnp.where(peer >= N, peer - N, peer)
-        pl.semaphore_signal(barrier, inc=1, device_id=(peer,), device_id_type=MESH)
-
     z, y, x, c = digits(me)
     zs = [((z + d) % 4) * 32 for d in range(4)]
     ys = [((y + d) % 4) * 8 for d in range(4)]
@@ -82,6 +77,12 @@
         return zs[a] + ys[b] + xs[e] + cs[f]
 
     order = send_order()
+    ball = [k for k in order if hops(k) <= 2]
+    middle = [k for k in order if 2 < hops(k) <= 4]
+    outer = [k for k in order if hops(k) > 4]
+    barrier = pltpu.get_barrier_semaphore()
+    for k in ball:
+        pl.semaphore_signal(barrier, inc=1, device_id=(peer_of(k),), device_id_type=MESH)
 
     rows = lists_ref.shape[1]
     owned = cent.shape[0]
@@ -122,25 +123,47 @@
         at = pl.ds(pl.multiple_of((s * N + me) * 8, 8), 8)
         recv[at, :] = send[at, :]
 
-    pl.semaphore_wait(barrier, N - 1)
-    for k in order:
+    pl.semaphore_wait(barrier, len(ball))
+    def send_meta(k):
         peer = peer_of(k)
         pltpu.make_async_remote_copy(
             src_ref=msend.at[pl.ds(peer, 1)], dst_ref=mrecv.at[pl.ds(me, 1)],
             send_sem=msem.at[0], recv_sem=msem.at[1], device_id=(peer,), device_id_type=MESH,
         ).start()
 
-    def send_slot(s, carry):
-        for k in order:
-            peer = peer_of(k)
-            pltpu.make_async_remote_copy(
-                src_ref=send.at[pl.ds(pl.multiple_of((s * N + peer) * 8, 8), 8)],
-                dst_ref=recv.at[pl.ds(pl.multiple_of((s * N + me) * 8, 8), 8)],
-                send_sem=ssem.at[0], recv_sem=rsem.at[s], device_id=(peer,), device_id_type=MESH,
-            ).start()
-        return carry
-
-    lax.fori_loop(0, SLOTS, send_slot, 0)
+    def send_row(s, k):
+        peer = peer_of(k)
+        pltpu.make_async_remote_copy(
+            src_ref=send.at[pl.ds(pl.multiple_of((s * N + peer) * 8, 8), 8)],
+            dst_ref=recv.at[pl.ds(pl.multiple_of((s * N + me) * 8, 8), 8)],
+            send_sem=ssem.at[0], recv_sem=rsem.at[s], device_id=(peer,), device_id_type=MESH,
+        ).start()
+
+    def send_rows(ks, first, end):
+        def slot(s, carry):
+            for k in ks:
+                send_row(s, k)
+            return carry
+
+        lax.fori_loop(first, end, slot, 0)
+
+    for k in ball:
+        pl.semaphore_signal(wider.at[0], inc=1, device_id=(peer_of(k),), device_id_type=MESH)
+    for k in ball:
+        send_meta(k)
+    send_rows(ball, 0, NEAR_SLOTS)
+    pl.semaphore_wait(wider.at[0], len(ball))
+    for k in ball:
+        pl.semaphore_signal(wider.at[1], inc=1, device_id=(peer_of(k),), device_id_type=MESH)
+    for k in middle:
+        send_meta(k)
+    send_rows(middle, 0, 1)
+    pl.semaphore_wait(wider.at[1], len(ball))
+    for k in outer:
+        send_meta(k)
+    send_rows(outer, 0, 1)
+    send_rows(outer + middle, 1, NEAR_SLOTS)
+    send_rows(order, NEAR_SLOTS, SLOTS)
 
     rot_copy.wait()
     for nb in range(width // 256):
@@ -265,6 +288,7 @@
             pltpu.SemaphoreType.DMA((1,)),
             pltpu.SemaphoreType.DMA((SLOTS,)),
             pltpu.SemaphoreType.DMA((2,)),
+            pltpu.SemaphoreType.REGULAR((2,)),
         ],
         compiler_params=pltpu.CompilerParams(
             collective_id=0, has_side_effects=True, vmem_limit_bytes=40 << 20

time: 39.9 us -> 38.9 us (0.975)
  Pallas kernels: 39.2 us -> 38.1 us
    pallas_call x1, Pallas kernels: 37.8 us -> 36.7 us  [local(): pl.pallas_call(kernel, name='exchange', out_shape=results, in_specs=[hbm]...]
where the time goes in v4:
time: 38.9 us; the launch traced here: 38.7 us
  Pallas kernels  38.1 us (98%)
  between operations  0.64 us (2%)
    pallas_call x1, Pallas kernels, local(): pl.pallas_call(kernel, name='exchange', out_shape=results, in_specs=[hbm]...  36.7 us
    pallas_call x1, Pallas kernels, local(): pl.pallas_call(write_out, name='write_out', out_shape=results, in_specs=[...  1.35 us

profile of v4, /device:TPU:1, one launch (start us, length us, event | category | flops | bytes accessed | tf_op | source)
XLA Modules:
  0.0 38.7 jit_solution(3213926686800498957)
XLA Ops:
  0.6 36.7 %exchange.1 = (f32[512,1024]{1,0:T(8,128)S(1)}, s32[1,512]{1,0:T(1,128)S(1)}, s32[1,512]{1,0:T(1,128)S(1)}) custom-call(s32[1,256]{1,0:T(1,128)} %bitcast.4, s32[1,256]{1,0:T(1,128)} %bitcast.5, f32[256,1024]{1,0:T(8,128)} %emb_hbm.1, f32[512,1024]{1,0:T(8,128)} %cent_hbm.1, f32[1024,1024]{1,0:T(8,128)} %rot_hbm.1), custom_call_target="tpu_custom_call" | custom-call | tf_op jit(solution)/shard_map/exchange/pallas_call | solution.py:266
  37.4 1.4 %write_out.1 = (f32[512,1024]{1,0:T(8,128)}, s32[1,512]{1,0:T(1,128)}, s32[1,512]{1,0:T(1,128)}) custom-call(f32[512,1024]{1,0:T(8,128)S(1)} %get-tuple-element.9.packed_vm, s32[1,512]{1,0:T(1,128)S(1)} %get-tuple-element.10.pids_vm, s32[1,512]{1,0:T(1,128)S(1)} %get-tuple-element.11.offs_vm), custom_call_target="tpu_custom_call" | custom-call | tf_op jit(solution)/shard_map/write_out/pallas_call | solution.py:297

commit v5 on v4

--- a/solution.py
+++ b/solution.py
@@ -15,6 +15,8 @@
 F32 = jnp.float32
 BF16 = jnp.bfloat16
 BIG = float(1 << 20)
+RADII = (2, 1, 1, 2)
+MID_SLOTS = 1
 NEAR_SLOTS = 3
 
 
@@ -77,11 +79,12 @@
         return zs[a] + ys[b] + xs[e] + cs[f]
 
     order = send_order()
-    ball = [k for k in order if hops(k) <= 2]
-    middle = [k for k in order if 2 < hops(k) <= 4]
-    outer = [k for k in order if hops(k) > 4]
+
+    def within(radius):
+        return [k for k in order if hops(k) <= radius]
+
     barrier = pltpu.get_barrier_semaphore()
-    for k in ball:
+    for k in within(RADII[0]):
         pl.semaphore_signal(barrier, inc=1, device_id=(peer_of(k),), device_id_type=MESH)
 
     rows = lists_ref.shape[1]
@@ -95,17 +98,8 @@
     mine = owner == iota((N, rows), 0)
     earlier = (iota((rows, rows), 0) < iota((rows, rows), 1)).astype(BF16)
     count = mm(mine.astype(BF16), earlier)
-    lane = iota((N, 128), 1)
-    meta = jnp.zeros((N, 128), F32)
-    picks = []
-    for s in range(SLOTS):
-        pick = mine & (count == float(s))
-        l_of = jnp.sum(jnp.where(pick, local + 1.0, 0.0), axis=1, keepdims=True) - 1.0
-        i_of = jnp.sum(jnp.where(pick, ids, 0.0), axis=1, keepdims=True)
-        meta = jnp.where(lane == s, l_of, meta)
-        meta = jnp.where(lane == SLOTS + s, i_of, meta)
-        picks.append(pick.astype(BF16))
-    msend[...] = meta.reshape(N, 1, 128)
+    masks = [mine & (count == float(s)) for s in range(SLOTS)]
+    picks = [v.astype(BF16) for v in masks]
     pick_all = jnp.concatenate(picks, axis=0)
 
     emb_copy.wait()
@@ -118,12 +112,11 @@
         for j in range(2):
             send[pl.ds(nb * 2 + j, SLOTS * N, stride=8), :] = out[:, j * 128:(j + 1) * 128]
 
-    mrecv[pl.ds(me, 1)] = msend[pl.ds(me, 1)]
     for s in range(SLOTS):
         at = pl.ds(pl.multiple_of((s * N + me) * 8, 8), 8)
         recv[at, :] = send[at, :]
 
-    pl.semaphore_wait(barrier, len(ball))
+    pl.semaphore_wait(barrier, len(within(RADII[0])))
     def send_meta(k):
         peer = peer_of(k)
         pltpu.make_async_remote_copy(
@@ -147,22 +140,40 @@
 
         lax.fori_loop(first, end, slot, 0)
 
-    for k in ball:
-        pl.semaphore_signal(wider.at[0], inc=1, device_id=(peer_of(k),), device_id_type=MESH)
-    for k in ball:
-        send_meta(k)
-    send_rows(ball, 0, NEAR_SLOTS)
-    pl.semaphore_wait(wider.at[0], len(ball))
-    for k in ball:
-        pl.semaphore_signal(wider.at[1], inc=1, device_id=(peer_of(k),), device_id_type=MESH)
-    for k in middle:
-        send_meta(k)
-    send_rows(middle, 0, 1)
-    pl.semaphore_wait(wider.at[1], len(ball))
-    for k in outer:
-        send_meta(k)
-    send_rows(outer, 0, 1)
-    send_rows(outer + middle, 1, NEAR_SLOTS)
+    def build_meta():
+        lane = iota((N, 128), 1)
+        meta = jnp.zeros((N, 128), F32)
+        for s, pick in enumerate(masks):
+            l_of = jnp.sum(jnp.where(pick, local + 1.0, 0.0), axis=1, keepdims=True) - 1.0
+            i_of = jnp.sum(jnp.where(pick, ids, 0.0), axis=1, keepdims=True)
+            meta = jnp.where(lane == s, l_of, meta)
+            meta = jnp.where(lane == SLOTS + s, i_of, meta)
+        msend[...] = meta.reshape(N, 1, 128)
+        mrecv[pl.ds(me, 1)] = msend[pl.ds(me, 1)]
+
+    def signal_round(i):
+        for k in within(RADII[i + 1]):
+            pl.semaphore_signal(wider.at[i], inc=1, device_id=(peer_of(k),), device_id_type=MESH)
+
+    rounds = len(RADII) - 1
+    reached, metas = 0, []
+    for i in range(rounds + 1):
+        if i:
+            pl.semaphore_wait(wider.at[i - 1], len(within(RADII[i])))
+        if i < rounds:
+            signal_round(i)
+        known = reached + RADII[i]
+        fresh = [k for k in order if reached - (not i) < hops(k) <= known]
+        send_rows(fresh, 0, NEAR_SLOTS if known <= 2 else MID_SLOTS)
+        if i == 0:
+            build_meta()
+        metas += fresh
+        if i:
+            for k in metas:
+                send_meta(k)
+            metas = []
+        reached = known
+    send_rows([k for k in order if hops(k) > 2], MID_SLOTS, NEAR_SLOTS)
     send_rows(order, NEAR_SLOTS, SLOTS)
 
     rot_copy.wait()
@@ -288,7 +299,7 @@
             pltpu.SemaphoreType.DMA((1,)),
             pltpu.SemaphoreType.DMA((SLOTS,)),
             pltpu.SemaphoreType.DMA((2,)),
-            pltpu.SemaphoreType.REGULAR((2,)),
+            pltpu.SemaphoreType.REGULAR((len(RADII) - 1,)),
         ],
         compiler_params=pltpu.CompilerParams(
             collective_id=0, has_side_effects=True, vmem_limit_bytes=40 << 20

time: 38.9 us -> 38.5 us (0.990)
  Pallas kernels: 38.1 us -> 37.7 us
where the time goes in v5:
time: 38.5 us; the launch traced here: 38.4 us
  Pallas kernels  37.7 us (98%)
  between operations  0.64 us (2%)
    pallas_call x1, Pallas kernels, local(): pl.pallas_call(kernel, name='exchange', out_shape=results, in_specs=[hbm]...  36.4 us
    pallas_call x1, Pallas kernels, local(): pl.pallas_call(write_out, name='write_out', out_shape=results, in_specs=[...  1.35 us

profile of v5, /device:TPU:1, one launch (start us, length us, event | category | flops | bytes accessed | tf_op | source)
XLA Modules:
  0.0 38.4 jit_solution(7658964857655228655)
XLA Ops:
  0.6 36.4 %exchange.1 = (f32[512,1024]{1,0:T(8,128)S(1)}, s32[1,512]{1,0:T(1,128)S(1)}, s32[1,512]{1,0:T(1,128)S(1)}) custom-call(s32[1,256]{1,0:T(1,128)} %bitcast.4, s32[1,256]{1,0:T(1,128)} %bitcast.5, f32[256,1024]{1,0:T(8,128)} %emb_hbm.1, f32[512,1024]{1,0:T(8,128)} %cent_hbm.1, f32[1024,1024]{1,0:T(8,128)} %rot_hbm.1), custom_call_target="tpu_custom_call" | custom-call | tf_op jit(solution)/shard_map/exchange/pallas_call | solution.py:277
  37.0 1.4 %write_out.1 = (f32[512,1024]{1,0:T(8,128)}, s32[1,512]{1,0:T(1,128)}, s32[1,512]{1,0:T(1,128)}) custom-call(f32[512,1024]{1,0:T(8,128)S(1)} %get-tuple-element.9.packed_vm, s32[1,512]{1,0:T(1,128)S(1)} %get-tuple-element.10.pids_vm, s32[1,512]{1,0:T(1,128)S(1)} %get-tuple-element.11.offs_vm), custom_call_target="tpu_custom_call" | custom-call | tf_op jit(solution)/shard_map/write_out/pallas_call | solution.py:308

commit v6 on v5

--- a/solution.py
+++ b/solution.py
@@ -15,7 +15,7 @@
 F32 = jnp.float32
 BF16 = jnp.bfloat16
 BIG = float(1 << 20)
-RADII = (2, 1, 1, 2)
+RADII = (2, 1, 3)
 MID_SLOTS = 1
 NEAR_SLOTS = 3
 

time: 38.5 us -> 38.4 us (level)
  no operation moved by 1% of the time
where the time goes in v6:
time: 38.4 us; the launch traced here: 38.3 us
  Pallas kernels  37.7 us (98%)
  between operations  0.64 us (2%)
    pallas_call x1, Pallas kernels, local(): pl.pallas_call(kernel, name='exchange', out_shape=results, in_specs=[hbm]...  36.3 us
    pallas_call x1, Pallas kernels, local(): pl.pallas_call(write_out, name='write_out', out_shape=results, in_specs=[...  1.35 us

profile of v6, /device:TPU:1, one launch (start us, length us, event | category | flops | bytes accessed | tf_op | source)
XLA Modules:
  0.0 38.3 jit_solution(8778576836343895759)
XLA Ops:
  0.6 36.3 %exchange.1 = (f32[512,1024]{1,0:T(8,128)S(1)}, s32[1,512]{1,0:T(1,128)S(1)}, s32[1,512]{1,0:T(1,128)S(1)}) custom-call(s32[1,256]{1,0:T(1,128)} %bitcast.4, s32[1,256]{1,0:T(1,128)} %bitcast.5, f32[256,1024]{1,0:T(8,128)} %emb_hbm.1, f32[512,1024]{1,0:T(8,128)} %cent_hbm.1, f32[1024,1024]{1,0:T(8,128)} %rot_hbm.1), custom_call_target="tpu_custom_call" | custom-call | tf_op jit(solution)/shard_map/exchange/pallas_call | solution.py:277
  37.0 1.4 %write_out.1 = (f32[512,1024]{1,0:T(8,128)}, s32[1,512]{1,0:T(1,128)}, s32[1,512]{1,0:T(1,128)}) custom-call(f32[512,1024]{1,0:T(8,128)S(1)} %get-tuple-element.9.packed_vm, s32[1,512]{1,0:T(1,128)S(1)} %get-tuple-element.10.pids_vm, s32[1,512]{1,0:T(1,128)S(1)} %get-tuple-element.11.offs_vm), custom_call_target="tpu_custom_call" | custom-call | tf_op jit(solution)/shard_map/write_out/pallas_call | solution.py:308
